TPU v7x, 32 devices: a whole 2x2x4 slice. The times are simulated.
32 devices in a mesh: groups: 2 (over y), dp: 4 (over z), tensor: 4 (over x, core).
Axes of the slice: x: 2, y: 2, z: 4, core: 2. Of those that a mesh axis runs over, the one named last changes fastest.
Arguments:
- patches: bfloat16 [8192, 1280], P(('groups', 'dp')), parts along dimension 0, may hold values from -64 to 64
- grids: int32 [8, 2], P(('groups', 'dp')), parts along dimension 0, may hold values from 16 to 32, as said below
- dest: int32 [8, 256], P(('groups', 'dp')), parts along dimension 0, may hold values from 0 to 1535, as said below
- norm_gain: float32 [1280], replicated, may hold values from 0.1 to 1.9
- qkv_weight: bfloat16 [3, 1280, 1280], P(None, None, 'tensor'), may hold values from -8 to 8
- qkv_bias: float32 [3, 1280], P(None, 'tensor'), may hold values from -3 to 3
- proj_weight: bfloat16 [1280, 1280], P('tensor'), may hold values from -0.15625 to 0.15625
- proj_bias: float32 [1280], replicated, may hold values from -3 to 3
- merge_gain: float32 [1280], replicated, may hold values from 0.1 to 1.9
- w_first: bfloat16 [5120, 5120], P('dp', 'tensor'), may hold values from -0.078125 to 0.078125
- b_first: float32 [5120], P('tensor'), may hold values from -3 to 3
- w_second: bfloat16 [5120, 8192], P('tensor', 'dp'), may hold values from -0.078125 to 0.078125
- b_second: float32 [8192], P('tensor'), may hold values from -3 to 3
- text_embed: bfloat16 [3072, 8192], P(('groups', 'dp'), 'tensor'), parts along dimension 0, may hold values from -6 to 6
Outputs:
- sequence: bfloat16 [3072, 8192], P(('groups', 'dp'), 'tensor'), parts along dimension 0
There are 2 independent parts, one for each index of `groups`. A program takes and returns all parts, laid end to end along the dimension named above; an argument that names none is the same for every part. Nothing has to cross between parts.
Inputs may be any that keep to these rules, and one draw needn't show every extreme that they name: `grids`: both sides of every grid are even, at least 16 and at most 32; in each part along `groups`, the first image (the one on dp index 0) has the full 32 x 32 grid. The rows dest[i, j] with j < grids[i, 0] * grids[i, 1] / 4 are distinct over all images; the live rows of one image reach at most 64 rows in each aligned block of 384 sequence rows, and exactly that many for a full grid.
All inputs are finite; a program needn't handle non-finite values.
Results may differ from a plain program's by a relative error of at most 0.014.
Values may be sent and summed in bfloat16 or wider, within the bound.
A program may use at most 128 MiB of HBM per device.

v0:
```python
import math
import jax
import jax.numpy as jnp
from jax import lax
from jax.sharding import PartitionSpec as P

HEAD_DIM = 80
PATCHES = 1024
MERGED = 256


def rms_scale(values, gain):
    return values * lax.rsqrt(jnp.mean(values * values, axis=-1, keepdims=True) + 1e-06) * gain


def local(
    patches,
    grids,
    dest,
    norm_gain,
    qkv_weight,
    qkv_bias,
    proj_weight,
    proj_bias,
    merge_gain,
    w_first,
    b_first,
    w_second,
    b_second,
    text_embed,
):
    rows_dev = patches.shape[0]
    images_dev = grids.shape[0]
    heads_dev = qkv_weight.shape[2] // HEAD_DIM
    live_count = grids[:, 0] * grids[:, 1]
    normed = rms_scale(patches.astype(jnp.float32), norm_gain).astype(jnp.bfloat16)
    projected = (
        jnp.einsum("rv,jvc->jrc", normed, qkv_weight, preferred_element_type=jnp.float32)
        + qkv_bias[:, None, :]
    )
    projected = projected.astype(jnp.bfloat16).reshape(3, images_dev, PATCHES, heads_dev, HEAD_DIM)
    scores = jnp.einsum(
        "iqhd,ikhd->ihqk", projected[0], projected[1], preferred_element_type=jnp.float32
    ) / math.sqrt(HEAD_DIM)
    live_keys = jnp.arange(PATCHES, dtype=jnp.int32)[None, :] < live_count[:, None]
    scores = jnp.where(live_keys[:, None, None, :], scores, jnp.float32(-1e30))
    peak_score = jnp.max(scores, axis=-1, keepdims=True)
    exponent = jnp.exp(scores - peak_score)
    weights = (exponent / jnp.sum(exponent, axis=-1, keepdims=True)).astype(jnp.bfloat16)
    attended = jnp.einsum(
        "ihqk,ikhd->iqhd", weights, projected[2], preferred_element_type=jnp.float32
    )
    attended = attended.astype(jnp.bfloat16).reshape(rows_dev, heads_dev * HEAD_DIM)
    partial_value = jnp.dot(attended, proj_weight, preferred_element_type=jnp.float32).astype(
        jnp.bfloat16
    )
    summed = lax.psum(partial_value, "tensor").astype(jnp.float32)
    resid = patches.astype(jnp.float32) + summed + proj_bias
    merged_in = rms_scale(resid, merge_gain).astype(jnp.bfloat16)
    merged_in = merged_in.reshape(rows_dev // 4, 4 * patches.shape[1])
    merged_dev = merged_in.shape[0]
    received = lax.all_to_all(merged_in, "dp", split_axis=1, concat_axis=0, tiled=True)
    first_out = lax.psum_scatter(
        jnp.dot(received, w_first, preferred_element_type=jnp.float32).astype(jnp.bfloat16),
        "dp",
        scatter_dimension=0,
        tiled=True,
    ).astype(jnp.float32)
    hidden = jax.nn.gelu(first_out + b_first, approximate=False).astype(jnp.bfloat16)
    second_rows = jnp.dot(
        hidden,
        lax.all_gather(w_second, "dp", axis=1, tiled=True),
        preferred_element_type=jnp.float32,
    ).astype(jnp.bfloat16)
    visual = lax.psum_scatter(second_rows, "tensor", scatter_dimension=1, tiled=True).astype(
        jnp.float32
    )
    visual = (visual + b_second).astype(jnp.bfloat16)
    feature_count = visual.shape[1]
    dp_count = lax.axis_size("dp")
    seq_rows = text_embed.shape[0]
    capacity = images_dev * (MERGED // dp_count)
    live_rows = (jnp.arange(MERGED, dtype=jnp.int32)[None, :] < (live_count // 4)[:, None]).reshape(
        merged_dev
    )
    dest_flat = dest.reshape(merged_dev)
    shard_id = jnp.where(live_rows, dest_flat // seq_rows, dp_count)
    local_row = dest_flat % seq_rows
    one_hot = (shard_id[:, None] == jnp.arange(dp_count, dtype=jnp.int32)[None, :]).astype(
        jnp.int32
    )
    before = jnp.cumsum(one_hot, axis=0) - one_hot
    slot_index = jnp.sum(before * one_hot, axis=1)
    buffer = (
        jnp.zeros((dp_count, capacity, feature_count), jnp.bfloat16)
        .at[shard_id, slot_index]
        .set(visual, mode="drop")
    )
    positions = (
        jnp.full((dp_count, capacity), seq_rows, jnp.int32)
        .at[shard_id, slot_index]
        .set(local_row, mode="drop")
    )
    arrived, arrived_rows = (
        lax.all_to_all(buffer, "dp", split_axis=0, concat_axis=0, tiled=True),
        lax.all_to_all(positions, "dp", split_axis=0, concat_axis=0, tiled=True),
    )
    sequence = text_embed.at[arrived_rows.reshape(-1)].set(
        arrived.reshape(-1, feature_count), mode="drop"
    )
    return sequence


def solution(mesh):
    in_specs = (
        P(("groups", "dp"), None),
        P(("groups", "dp"), None),
        P(("groups", "dp"), None),
        P(),
        P(None, None, "tensor"),
        P(None, "tensor"),
        P("tensor", None),
        P(),
        P(),
        P("dp", "tensor"),
        P("tensor"),
        P("tensor", "dp"),
        P("tensor"),
        P(("groups", "dp"), "tensor"),
    )
    out_specs = P(("groups", "dp"), "tensor")
    return jax.shard_map(local, mesh=mesh, in_specs=in_specs, out_specs=out_specs, check_vma=False)
```

profile of v0, /device:TPU:0, one launch (start us, length us, event | category | flops | bytes accessed | tf_op | source)
XLA Modules:
  0.0 749.1 jit_solution(11529100986900097305)
XLA Ops:
  6.5 2.9 copy.35
  9.4 0.7 fusion.104
  11.4 0.0 copy-start.10
  11.4 0.0 copy-start.12
  11.4 0.6 fusion.6
  12.0 1.1 copy-done.10
  13.1 2.9 fusion.15
  15.9 1.3 fusion.103
  17.3 10.9 %fusion.105 = (f32[4,1024]{1,0:T(4,128)S(1)}, f32[4,1024,1024]{1,2,0:T(8,128)}) fusion(pred[1024]{0:T(1024)(128)(4,1)S(1)} %iota_compare_fusion, bf16[1024,4,80]{0,2,1:T(8,128)(2,1)} %bitcast.76, bf16[1024,4,80]{0,2,1:T(8,128)(2,1)} %bitcast.75), kind=kOutput, calls=%fused_computation.150 | convolution fusion | flops 687866880 | bytes 18105344 | tf_op jit(solution)/shard_map/sub | solution.py:48
  28.1 7.6 %fusion.20 = bf16[4,80,1024]{2,1,0:T(8,128)(2,1)S(1)} fusion(bf16[1024,4,80]{0,2,1:T(8,128)(2,1)} %bitcast.74, f32[4,1024,1024]{1,2,0:T(8,128)} %get-tuple-element.17, f32[4,1024]{1,0:T(4,128)S(1)} %get-tuple-element.16), kind=kOutput, calls=%fused_computation.33 | convolution fusion | flops 679804928 | bytes 18104320 | tf_op jit(solution)/shard_map/ihqk,ikhd->iqhd/dot_general | solution.py:50
  35.8 3.1 convolution_convert_fusion.2
  38.9 0.0 all-reduce.2.cloned.1.call-update
  38.9 0.2 reduce-scatter.3.cloned.1.call-start
  39.1 62.5 %all-reduce.2.cloned.1.call-done = bf16[1024,1280]{1,0:T(8,128)(2,1)} async-done(((bf16[1024,1280]{1,0:T(8,128)(2,1)}), bf16[1024,1280]{1,0:T(8,128)(2,1)}) %all-reduce.2.cloned.1.call-update) | async-done | bytes 2621456 | tf_op jit(solution)/shard_map/psum | solution.py:57
  101.7 3.8 multiply_reduce_fusion
  105.5 0.3 copy-done.4
  105.8 2.6 multiply_convert_fusion
  108.4 5.6 all_to_all.25
  114.0 2.1 copy.26
  116.0 63.6 %all_to_all.33 = bf16[256,4,1280]{2,0,1:T(8,128)(2,1)S(1)} all-to-all(bf16[256,4,1280]{2,0,1:T(8,128)(2,1)S(1)} %copy.26), channel_id=1, replica_groups=mesh['groups'=2,'dp'=4,'tensor'=4] {'dp'}, dimensions={1} | all-to-all | bytes 5242880 | tf_op jit(solution)/shard_map/all_to_all | solution.py:62
  179.6 4.9 convolution_convert_fusion.1
  184.5 0.0 reduce-scatter.3.cloned.1.call-update
  184.5 0.0 all-gather.2.cloned.1.call-start
  184.5 0.7 all-gather.2.cloned.1.call-update
  185.2 0.0 reduce-scatter.5.cloned.1.call-start
  185.3 50.0 %reduce-scatter.3.cloned.1.call-done = bf16[256,1280]{1,0:T(8,128)(2,1)} async-done(((bf16[1024,1280]{1,0:T(8,128)(2,1)}), bf16[256,1280]{1,0:T(8,128)(2,1)}) %reduce-scatter.3.cloned.1.call-update) | async-done | bytes 655376 | tf_op jit(solution)/shard_map/reduce_scatter | solution.py:63
  235.3 358.0 %all-gather.2.cloned.1.call-done = bf16[1280,8192]{1,0:T(8,128)(2,1)} async-done(((bf16[1280,2048]{1,0:T(8,128)(2,1)}), bf16[1280,8192]{1,0:T(8,128)(2,1)}) %all-gather.2.cloned.1.call-update) | async-done | bytes 20971536 | tf_op jit(solution)/shard_map/all_gather | solution.py:72
  593.3 17.4 %convolution_convert_fusion = bf16[256,8192]{1,0:T(8,128)(2,1)} fusion(bf16[1280,8192]{1,0:T(8,128)(2,1)} %all-gather.2.cloned.1.call-done, bf16[256,1280]{1,0:T(8,128)(2,1)} %reduce-scatter.3.cloned.1.call-done, f32[1280]{0:T(1024)S(1)} %copy-done.13), kind=kOutput, calls=%fused_computation.8 | convolution fusion | flops 5392760832 | bytes 25826304 | tf_op jit(solution)/shard_map/dot_general | solution.py:70
  610.7 0.0 reduce-scatter.5.cloned.1.call-update
  610.7 0.6 copy-done.6
  611.4 1.2 reduce-window.6
  612.7 0.1 slice.35
  612.7 0.1 copy.22
  612.9 0.1 copy.23
  613.0 0.1 add_bitcast_fusion
  613.1 0.6 broadcast_in_dim.23
  613.7 38.8 %scatter_fusion = s32[4,64]{1,0:T(4,128)} fusion(s32[4,64]{1,0:T(4,128)} %broadcast_in_dim.23, s32[256]{0:T(256)S(1)} %bitcast.71, s32[256]{0:T(256)S(1)} %get-tuple-element.10), kind=kCustom, calls=%fused_computation | custom fusion | bytes 5120 | tf_op jit(solution)/shard_map/scatter | solution.py:102
  652.5 3.2 all-to-all-start
  655.7 0.0 reduce-scatter.5.cloned.1.call-done
  655.7 1.5 add_convert_fusion.1
  657.2 1.2 broadcast_in_dim.28
  658.4 48.1 %scatter_fusion.1 = bf16[4,64,2048]{2,1,0:T(8,128)(2,1)} fusion(bf16[4,64,2048]{2,1,0:T(8,128)(2,1)} %broadcast_in_dim.28, s32[256]{0:T(256)S(1)} %bitcast.72, bf16[256,2048]{1,0:T(8,128)(2,1)S(1)} %add_convert_fusion.1), kind=kCustom, calls=%fused_computation.1 | custom fusion | bytes 3147776 | tf_op jit(solution)/shard_map/scatter | solution.py:97
  706.5 5.0 all-to-all-start.2
  711.5 0.5 broadcast.284
  712.0 0.6 reduce.11
  712.7 0.1 reshape.264
  712.8 24.2 %all-to-all-done.2 = bf16[4,64,2048]{2,1,0:T(8,128)(2,1)} async-done(((bf16[4,64,2048]{2,1,0:T(8,128)(2,1)}), bf16[4,64,2048]{2,1,0:T(8,128)(2,1)}, u32[]{:S(2)}, u32[]{:S(2)}) %all-to-all-start.2) | async-done | bytes 1048608 | tf_op jit(solution)/shard_map/all_to_all | solution.py:105
  736.9 5.7 scatter_fusion.2
  (40 shorter events, 0.2 us)
Async XLA Ops:
  6.5 173.1 %copy-start = (bf16[1280,1280]{1,0:T(8,128)(2,1)S(1)}, bf16[1280,1280]{1,0:T(8,128)(2,1)}, u32[]{:S(2)}) copy-start(bf16[1280,1280]{1,0:T(8,128)(2,1)} %param.23) | copy-start | bytes 9830404
  6.5 2.9 copy-start.9
  6.5 95.1 %all-reduce.2.cloned.1.call-start = ((), (), s32[]{:S(2)}) async-start(), calls=%async_computation.5 | async-start | bytes 5242880 | tf_op jit(solution)/shard_map/psum | solution.py:57
  6.5 4.8 copy-start.2
  11.4 1.7 copy-start.10
  11.4 1.7 copy-start.12
  11.4 1.7 copy-start.14
  28.1 7.6 %copy-start.11 = (bf16[320,1280]{1,0:T(8,128)(2,1)S(1)}, bf16[320,1280]{1,0:T(8,128)(2,1)}, u32[]{:S(2)}) copy-start(bf16[320,1280]{1,0:T(8,128)(2,1)} %param.20) | copy-start | bytes 2457604
  38.9 62.8 %copy-start.5 = (f32[1280]{0:T(1024)S(1)}, f32[1280]{0:T(1024)}, u32[]{:S(2)}) copy-start(f32[1280]{0:T(1024)} %param.21) | copy-start | bytes 15364
  38.9 66.6 %copy-start.7 = (f32[1280]{0:T(1024)S(1)}, f32[1280]{0:T(1024)}, u32[]{:S(2)}) copy-start(f32[1280]{0:T(1024)} %param.22) | copy-start | bytes 15364
  38.9 196.4 %reduce-scatter.3.cloned.1.call-start = ((), (), s32[]{:S(2)}) async-start(), calls=%async_computation.6 | async-start | bytes 3276800 | tf_op jit(solution)/shard_map/reduce_scatter | solution.py:63
  101.7 3.8 copy-start.3
  101.7 4.1 copy-start.4
  184.5 408.8 %copy-start.13 = (f32[1280]{0:T(1024)S(1)}, f32[1280]{0:T(1024)}, u32[]{:S(2)}) copy-start(f32[1280]{0:T(1024)} %param.24) | copy-start | bytes 15364
  184.5 408.8 %all-gather.2.cloned.1.call-start = ((), (), s32[]{:S(2)}) async-start(), calls=%async_computation.7 | async-start | bytes 26214400 | tf_op jit(solution)/shard_map/all_gather | solution.py:72
  185.2 470.5 %reduce-scatter.5.cloned.1.call-start = ((), (), s32[]{:S(2)}) async-start(), calls=%async_computation.8 | async-start | bytes 5242880 | tf_op jit(solution)/shard_map/reduce_scatter | solution.py:75
  610.7 0.7 copy-start.6
  610.7 45.0 %copy-start.8 = (f32[2048]{0:T(1024)S(1)}, f32[2048]{0:T(1024)}, u32[]{:S(2)}) copy-start(f32[2048]{0:T(1024)} %param.26) | copy-start | bytes 24580
  652.5 54.0 %all-to-all-start = ((s32[4,1,64]{2,1,0:T(1,128)}), s32[4,1,64]{2,1,0:T(1,128)S(1)}, u32[]{:S(2)}, u32[]{:S(2)}) async-start(s32[4,1,64]{2,1,0:T(1,128)} %bitcast.12), calls=%async_computation | async-start | bytes 4096 | tf_op jit(solution)/shard_map/all_to_all | solution.py:106
  706.5 30.4 %all-to-all-start.2 = ((bf16[4,64,2048]{2,1,0:T(8,128)(2,1)}), bf16[4,64,2048]{2,1,0:T(8,128)(2,1)}, u32[]{:S(2)}, u32[]{:S(2)}) async-start(bf16[4,64,2048]{2,1,0:T(8,128)(2,1)} %scatter_fusion.1), calls=%async_computation.4 | async-start | bytes 2097152 | tf_op jit(solution)/shard_map/all_to_all | solution.py:105
  736.9 5.7 copy-start.1
Sparse Core Ops, SparseCore 0:
  39.0 62.6 all-reduce.1
  184.6 50.6 reduce-scatter.2
  236.9 356.3 all-gather.1
  610.8 42.9 reduce-scatter.4
where the time goes:
time: 753 us; the launch traced here: 749 us
  waiting for transfers between devices  495 us (66%)
  local copies, waits for them, and re-layouts  110 us (15%)
  blocking collectives  63.6 us (8%)
  matrix products  46.7 us (6%)
  between operations  14.6 us (2%)
  other arithmetic  10.6 us (1%)
  starting transfers between devices  8.51 us (1%)
    all_gather x1, waiting for transfers between devices, local(): lax.all_gather(w_second, 'dp', axis=1, tiled=True)  358 us
    all_to_all x1, blocking collectives, local(): lax.all_to_all(merged_in, 'dp', split_axis=1, concat_axis=0, tiled=True)  63.6 us
    psum x1, waiting for transfers between devices, local(): summed = lax.psum(partial_value, 'tensor').astype(jnp.float32)  62.5 us
    reduce_scatter x1, waiting for transfers between devices, local(): lax.psum_scatter(jnp.dot(received, w_first, preferred_element_type=jnp.fl...  50 us
    scatter x1, local copies, waits for them, and re-layouts, local(): buffer = jnp.zeros((dp_count, capacity, feature_count), jnp.bfloat16).at[...  48.1 us
    scatter x1, local copies, waits for them, and re-layouts, local(): positions = jnp.full((dp_count, capacity), seq_rows, jnp.int32).at[shard_...  38.8 us
    all_to_all x1, waiting for transfers between devices, local(): lax.all_to_all(buffer, 'dp', split_axis=0, concat_axis=0, tiled=True)  24.2 us
    dot_general x1, matrix products, local(): jnp.dot(hidden, lax.all_gather(w_second, 'dp', axis=1, tiled=True), prefe...  17.4 us
  transfers between devices with their start and end apart: 6, of which 4 were waited for; matrix products, arithmetic and copies ran while one was open for 12% of the time, Pallas kernels for 0%

commit v1 on v0

--- a/solution.py
+++ b/solution.py
@@ -59,7 +59,9 @@
     merged_in = rms_scale(resid, merge_gain).astype(jnp.bfloat16)
     merged_in = merged_in.reshape(rows_dev // 4, 4 * patches.shape[1])
     merged_dev = merged_in.shape[0]
-    received = lax.all_to_all(merged_in, "dp", split_axis=1, concat_axis=0, tiled=True)
+    pieces = jnp.split(merged_in, lax.axis_size("dp"), axis=1)
+    incoming = lax.all_to_all(jnp.stack(pieces), "dp", 0, 0)
+    received = jnp.concatenate(incoming, axis=0)
     first_out = lax.psum_scatter(
         jnp.dot(received, w_first, preferred_element_type=jnp.float32).astype(jnp.bfloat16),
         "dp",

time: 753 us -> 751 us (level)
    all_to_all x2 -> x0, local copies, waits for them, and re-layouts: 7.62 us -> none  [local(): lax.all_to_all(merged_in, 'dp', split_axis=1, concat_axis=0, tiled=True)]
where the time goes in v1:
time: 751 us; the launch traced here: 748 us
  waiting for transfers between devices  495 us (66%)
  local copies, waits for them, and re-layouts  108 us (14%)
  blocking collectives  63.6 us (8%)
  matrix products  46.7 us (6%)
  between operations  14.7 us (2%)
  other arithmetic  10.9 us (1%)
  starting transfers between devices  8.51 us (1%)
    all_gather x1, waiting for transfers between devices, local(): lax.all_gather(w_second, 'dp', axis=1, tiled=True)  358 us
    all_to_all x1, blocking collectives, local(): incoming = lax.all_to_all(jnp.stack(pieces), 'dp', 0, 0)  63.6 us
    psum x1, waiting for transfers between devices, local(): summed = lax.psum(partial_value, 'tensor').astype(jnp.float32)  62.6 us
    reduce_scatter x1, waiting for transfers between devices, local(): lax.psum_scatter(jnp.dot(received, w_first, preferred_element_type=jnp.fl...  50 us
    scatter x1, local copies, waits for them, and re-layouts, local(): buffer = jnp.zeros((dp_count, capacity, feature_count), jnp.bfloat16).at[...  48.1 us
    scatter x1, local copies, waits for them, and re-layouts, local(): positions = jnp.full((dp_count, capacity), seq_rows, jnp.int32).at[shard_...  38.8 us
    all_to_all x1, waiting for transfers between devices, local(): lax.all_to_all(buffer, 'dp', split_axis=0, concat_axis=0, tiled=True)  24.2 us
    dot_general x1, matrix products, local(): jnp.dot(hidden, lax.all_gather(w_second, 'dp', axis=1, tiled=True), prefe...  17.4 us
  transfers between devices with their start and end apart: 6, of which 4 were waited for; matrix products, arithmetic and copies ran while one was open for 12% of the time, Pallas kernels for 0%

profile of v1, /device:TPU:0, one launch (start us, length us, event | category | flops | bytes accessed | tf_op | source)
XLA Modules:
  0.0 748.0 jit_solution(11138553657485548527)
XLA Ops:
  6.5 2.9 copy.30
  9.4 0.7 fusion.104
  11.5 0.6 fusion.6
  12.1 2.9 fusion.15
  15.0 1.3 fusion.103
  16.3 10.9 %fusion.105 = (f32[4,1024]{1,0:T(4,128)S(1)}, f32[4,1024,1024]{1,2,0:T(8,128)}) fusion(pred[1024]{0:T(1024)(128)(4,1)S(1)} %iota_compare_fusion, bf16[1024,4,80]{0,2,1:T(8,128)(2,1)} %bitcast.82, bf16[1024,4,80]{0,2,1:T(8,128)(2,1)} %bitcast.81), kind=kOutput, calls=%fused_computation.155 | convolution fusion | flops 687866880 | bytes 18105344 | tf_op jit(solution)/shard_map/sub | solution.py:48
  27.2 7.6 %fusion.20 = bf16[4,80,1024]{2,1,0:T(8,128)(2,1)S(1)} fusion(bf16[1024,4,80]{0,2,1:T(8,128)(2,1)} %bitcast.80, f32[4,1024,1024]{1,2,0:T(8,128)} %get-tuple-element.21, f32[4,1024]{1,0:T(4,128)S(1)} %get-tuple-element.20), kind=kOutput, calls=%fused_computation.34 | convolution fusion | flops 679804928 | bytes 18104320 | tf_op jit(solution)/shard_map/ihqk,ikhd->iqhd/dot_general | solution.py:50
  34.8 3.1 convolution_convert_fusion.2
  37.9 0.0 all-reduce.2.cloned.1.call-update
  37.9 0.0 copy-start.7
  37.9 0.2 reduce-scatter.3.cloned.1.call-start
  38.2 62.6 %all-reduce.2.cloned.1.call-done = bf16[1024,1280]{1,0:T(8,128)(2,1)} async-done(((bf16[1024,1280]{1,0:T(8,128)(2,1)}), bf16[1024,1280]{1,0:T(8,128)(2,1)}) %all-reduce.2.cloned.1.call-update) | async-done | bytes 2621456 | tf_op jit(solution)/shard_map/psum | solution.py:57
  100.7 3.8 multiply_reduce_fusion
  104.5 0.3 copy-done.4
  104.8 2.6 multiply_convert_fusion
  107.4 5.2 reshape.270
  112.7 1.9 slice_bitcast_fusion.3
  114.5 0.3 pad_maximum_fusion
  114.9 63.6 %all_to_all.19 = bf16[4,256,1280]{2,1,0:T(8,128)(2,1)S(1)} all-to-all(bf16[4,256,1280]{2,1,0:T(8,128)(2,1)S(1)} %pad_maximum_fusion), channel_id=1, replica_groups=mesh['groups'=2,'dp'=4,'tensor'=4] {'dp'}, dimensions={0} | all-to-all | bytes 5242880 | tf_op jit(solution)/shard_map/all_to_all | solution.py:63
  178.4 4.9 convolution_convert_fusion.1
  183.3 0.0 reduce-scatter.3.cloned.1.call-update
  183.3 0.0 copy-start.13
  183.3 0.0 all-gather.2.cloned.1.call-start
  183.4 0.7 all-gather.2.cloned.1.call-update
  184.1 0.0 reduce-scatter.5.cloned.1.call-start
  184.1 50.0 %reduce-scatter.3.cloned.1.call-done = bf16[256,1280]{1,0:T(8,128)(2,1)} async-done(((bf16[1024,1280]{1,0:T(8,128)(2,1)}), bf16[256,1280]{1,0:T(8,128)(2,1)}) %reduce-scatter.3.cloned.1.call-update) | async-done | bytes 655376 | tf_op jit(solution)/shard_map/reduce_scatter | solution.py:65
  234.1 358.0 %all-gather.2.cloned.1.call-done = bf16[1280,8192]{1,0:T(8,128)(2,1)} async-done(((bf16[1280,2048]{1,0:T(8,128)(2,1)}), bf16[1280,8192]{1,0:T(8,128)(2,1)}) %all-gather.2.cloned.1.call-update) | async-done | bytes 20971536 | tf_op jit(solution)/shard_map/all_gather | solution.py:74
  592.2 17.4 %convolution_convert_fusion = bf16[256,8192]{1,0:T(8,128)(2,1)} fusion(bf16[1280,8192]{1,0:T(8,128)(2,1)} %all-gather.2.cloned.1.call-done, bf16[256,1280]{1,0:T(8,128)(2,1)} %reduce-scatter.3.cloned.1.call-done, f32[1280]{0:T(1024)S(1)} %copy-done.13), kind=kOutput, calls=%fused_computation.8 | convolution fusion | flops 5392760832 | bytes 25826304 | tf_op jit(solution)/shard_map/dot_general | solution.py:72
  609.5 0.0 reduce-scatter.5.cloned.1.call-update
  609.6 0.6 copy-done.6
  610.3 1.2 reduce-window.6
  611.5 0.1 slice.35
  611.6 0.1 copy.18
  611.7 0.1 copy.19
  611.8 0.1 add_bitcast_fusion
  612.0 0.6 broadcast_in_dim.23
  612.5 38.8 %scatter_fusion = s32[4,64]{1,0:T(4,128)} fusion(s32[4,64]{1,0:T(4,128)} %broadcast_in_dim.23, s32[256]{0:T(256)S(1)} %bitcast.77, s32[256]{0:T(256)S(1)} %get-tuple-element.14), kind=kCustom, calls=%fused_computation | custom fusion | bytes 5120 | tf_op jit(solution)/shard_map/scatter | solution.py:104
  651.3 3.2 all-to-all-start
  654.5 0.0 reduce-scatter.5.cloned.1.call-done
  654.6 1.5 add_convert_fusion.1
  656.1 1.2 broadcast_in_dim.28
  657.2 48.1 %scatter_fusion.1 = bf16[4,64,2048]{2,1,0:T(8,128)(2,1)} fusion(bf16[4,64,2048]{2,1,0:T(8,128)(2,1)} %broadcast_in_dim.28, s32[256]{0:T(256)S(1)} %bitcast.78, bf16[256,2048]{1,0:T(8,128)(2,1)S(1)} %add_convert_fusion.1), kind=kCustom, calls=%fused_computation.1 | custom fusion | bytes 3147776 | tf_op jit(solution)/shard_map/scatter | solution.py:99
  705.3 5.0 all-to-all-start.2
  710.4 0.5 broadcast.284
  710.9 0.6 reduce.11
  711.5 0.1 reshape.265
  711.6 24.2 %all-to-all-done.2 = bf16[4,64,2048]{2,1,0:T(8,128)(2,1)} async-done(((bf16[4,64,2048]{2,1,0:T(8,128)(2,1)}), bf16[4,64,2048]{2,1,0:T(8,128)(2,1)}, u32[]{:S(2)}, u32[]{:S(2)}) %all-to-all-start.2) | async-done | bytes 1048608 | tf_op jit(solution)/shard_map/all_to_all | solution.py:107
  735.8 5.7 scatter_fusion.2
  (41 shorter events, 0.2 us)
Async XLA Ops:
  6.5 171.9 %copy-start = (bf16[1280,1280]{1,0:T(8,128)(2,1)S(1)}, bf16[1280,1280]{1,0:T(8,128)(2,1)}, u32[]{:S(2)}) copy-start(bf16[1280,1280]{1,0:T(8,128)(2,1)} %param.23) | copy-start | bytes 9830404
  6.5 2.9 copy-start.9
  6.5 94.2 %all-reduce.2.cloned.1.call-start = ((), (), s32[]{:S(2)}) async-start(), calls=%async_computation.5 | async-start | bytes 5242880 | tf_op jit(solution)/shard_map/psum | solution.py:57
  6.5 4.9 copy-start.2
  9.4 2.6 copy-start.10
  9.4 2.7 copy-start.12
  9.4 2.7 copy-start.14
  27.2 7.6 %copy-start.11 = (bf16[320,1280]{1,0:T(8,128)(2,1)S(1)}, bf16[320,1280]{1,0:T(8,128)(2,1)}, u32[]{:S(2)}) copy-start(bf16[320,1280]{1,0:T(8,128)(2,1)} %param.20) | copy-start | bytes 2457604
  37.9 62.8 %copy-start.5 = (f32[1280]{0:T(1024)S(1)}, f32[1280]{0:T(1024)}, u32[]{:S(2)}) copy-start(f32[1280]{0:T(1024)} %param.21) | copy-start | bytes 15364
  37.9 66.6 %copy-start.7 = (f32[1280]{0:T(1024)S(1)}, f32[1280]{0:T(1024)}, u32[]{:S(2)}) copy-start(f32[1280]{0:T(1024)} %param.22) | copy-start | bytes 15364
  37.9 196.2 %reduce-scatter.3.cloned.1.call-start = ((), (), s32[]{:S(2)}) async-start(), calls=%async_computation.6 | async-start | bytes 3276800 | tf_op jit(solution)/shard_map/reduce_scatter | solution.py:65
  100.7 3.8 copy-start.3
  100.7 4.1 copy-start.4
  183.3 408.8 %copy-start.13 = (f32[1280]{0:T(1024)S(1)}, f32[1280]{0:T(1024)}, u32[]{:S(2)}) copy-start(f32[1280]{0:T(1024)} %param.24) | copy-start | bytes 15364
  183.3 408.8 %all-gather.2.cloned.1.call-start = ((), (), s32[]{:S(2)}) async-start(), calls=%async_computation.7 | async-start | bytes 26214400 | tf_op jit(solution)/shard_map/all_gather | solution.py:74
  184.1 470.5 %reduce-scatter.5.cloned.1.call-start = ((), (), s32[]{:S(2)}) async-start(), calls=%async_computation.8 | async-start | bytes 5242880 | tf_op jit(solution)/shard_map/reduce_scatter | solution.py:77
  609.5 0.7 copy-start.6
  609.6 45.0 %copy-start.8 = (f32[2048]{0:T(1024)S(1)}, f32[2048]{0:T(1024)}, u32[]{:S(2)}) copy-start(f32[2048]{0:T(1024)} %param.26) | copy-start | bytes 24580
  651.3 54.0 %all-to-all-start = ((s32[4,1,64]{2,1,0:T(1,128)}), s32[4,1,64]{2,1,0:T(1,128)S(1)}, u32[]{:S(2)}, u32[]{:S(2)}) async-start(s32[4,1,64]{2,1,0:T(1,128)} %bitcast.12), calls=%async_computation | async-start | bytes 4096 | tf_op jit(solution)/shard_map/all_to_all | solution.py:108
  705.3 30.4 %all-to-all-start.2 = ((bf16[4,64,2048]{2,1,0:T(8,128)(2,1)}), bf16[4,64,2048]{2,1,0:T(8,128)(2,1)}, u32[]{:S(2)}, u32[]{:S(2)}) async-start(bf16[4,64,2048]{2,1,0:T(8,128)(2,1)} %scatter_fusion.1), calls=%async_computation.4 | async-start | bytes 2097152 | tf_op jit(solution)/shard_map/all_to_all | solution.py:107
  735.8 5.7 copy-start.1
Sparse Core Ops, SparseCore 0:
  38.0 62.6 all-reduce.1
  183.4 50.6 reduce-scatter.2
  235.7 356.3 all-gather.1
  609.7 42.9 reduce-scatter.4
